TPU v7x, 32 devices: a whole 2x2x4 slice. The times are simulated.
32 devices in a mesh: row: 4 (over y, core), col: 4 (over z), dp: 2 (over x).
Axes of the slice: x: 2, y: 2, z: 4, core: 2. Of those that a mesh axis runs over, the one named last changes fastest.
Arguments:
- slides: bfloat16 [2, 64, 128, 512], P('dp', 'row', 'col'), may hold values from -6 to 6
- cotangent: bfloat16 [2, 64, 128, 512], P('dp', 'row', 'col'), may hold values from -6 to 6
- kernel: float32 [2, 7, 7, 512], replicated, may hold values from -0.875 to 0.875
- kernel_bias: float32 [2, 512], replicated, may hold values from -3 to 3
- norm_gain: float32 [2, 512], replicated, may hold values from 0.1 to 1.9
- norm_bias: float32 [2, 512], replicated, may hold values from -3 to 3
- weight_in: bfloat16 [2, 512, 2048], P(None, 'dp'), may hold values from -0.25 to 0.25
- bias_in: float32 [2, 2048], replicated, may hold values from -3 to 3
- weight_out: bfloat16 [2, 2048, 512], P(None, None, 'dp'), may hold values from -0.125 to 0.125
- bias_out: float32 [2, 512], replicated, may hold values from -3 to 3
- layer_scale: float32 [2, 512], replicated, may hold values from 0.3 to 1.5
Outputs:
- output: bfloat16 [2, 64, 128, 512], P('dp', 'row', 'col')
- grad_slides: bfloat16 [2, 64, 128, 512], P('dp', 'row', 'col')
- grad_weight_in: float32 [2, 512, 2048], P(None, 'dp')
- grad_weight_out: float32 [2, 2048, 512], P(None, None, 'dp')
- grad_kernel: float32 [2, 7, 7, 512], replicated
- grad_channel: float32 [2, 5, 512], replicated
- grad_bias_in: float32 [2, 2048], replicated
All inputs are finite; a program needn't handle non-finite values.
Results may differ from a plain program's by a relative error of at most 0.01.
Values may be sent and summed in bfloat16 or wider, within the bound.
A program may use at most 128 MiB of HBM per device.

v0:
```python
import functools

import jax
import jax.numpy as jnp
from jax import lax
from jax.experimental import pallas as pl
from jax.experimental.pallas import tpu as pltpu
from jax.sharding import PartitionSpec as P

COEF = 0.7978845608028654
CUBIC = 0.044715
EPSILON = 1e-06
LANES = 128
UNIT = 16
LEFT = 8
QUARTERS = 4
MESH = pl.DeviceIdType.MESH
F32 = jnp.float32
BF16 = jnp.bfloat16
STRAIGHT = ((-1, 0), (1, 0), (0, -1), (0, 1))
DIAGONAL = ((-1, -1), (-1, 1), (1, -1), (1, 1))
ROWS = (((0,), (0,)), ((), ()))
COLS = (((1,), (1,)), ((), ()))


def step_body(
    sizes,
    slides,
    cotangent,
    kernel,
    kernel_bias,
    norm_gain,
    norm_bias,
    weight_in,
    bias_in,
    weight_out,
    bias_out,
    layer_scale,
    output,
    grad_slides,
    out_in,
    out_out,
    out_small,
    pads,
    gpad,
    taps,
    mixed,
    win,
    wout,
    normed,
    rstd,
    normal,
    act,
    slope,
    branch,
    upstream,
    gb_low,
    gnorm,
    gbias,
    mixed_bias,
    grads,
    from_core,
    from_dp,
    from_row,
    from_col,
    final,
    small,
    small_row,
    small_cd,
    small_out,
    row_send,
    col_send,
    cor_send,
    row_recv,
    col_recv,
    cor_recv,
    cor_wide,
    sem_local,
    sem_ws,
    sem_wr,
    sem_hs,
    sem_hr,
    sem_gs,
    sem_gr,
    sem_ss,
    sem_sr,
    sem_out,
):
    R, C, DP = sizes["row"], sizes["col"], sizes["dp"]
    CD = C * DP
    L, NT, _, T, D = wout.shape[0], wout.shape[1], 0, wout.shape[2], wout.shape[3]
    J = D // LANES
    H, W = slides.shape[1], slides.shape[2]
    N = H * W
    DH = D // DP
    UN = DH // UNIT
    row, col, dp = lax.axis_index("row"), lax.axis_index("col"), lax.axis_index("dp")
    cd = col * DP + dp
    core = row % 2

    def remote(src, dst, ssem, rsem, **where):
        return pltpu.make_async_remote_copy(
            src_ref=src,
            dst_ref=dst,
            send_sem=ssem,
            recv_sem=rsem,
            device_id=where,
            device_id_type=MESH,
        )

    def flip(index, bit):
        return index + bit - 2 * bit * ((index // bit) % 2)

    def there(dr, dc):
        ok = True
        if dr:
            ok = (row > 0) if dr < 0 else (row < R - 1)
        if dc:
            side = (col > 0) if dc < 0 else (col < C - 1)
            ok = side if ok is True else jnp.logical_and(ok, side)
        return ok

    def cd_peer(k):
        peer = (cd + k) % CD
        return peer, peer // DP, peer % DP

    barrier = pltpu.get_barrier_semaphore()
    for k in range(1, R):
        pl.semaphore_signal(
            barrier, inc=1, device_id={"row": (row + k) % R}, device_id_type=MESH
        )
    for k in range(1, CD):
        _, pc, pd = cd_peer(k)
        pl.semaphore_signal(
            barrier, inc=1, device_id={"col": pc, "dp": pd}, device_id_type=MESH
        )
    for dr, dc in DIAGONAL:

        @pl.when(there(dr, dc))
        def _():
            pl.semaphore_signal(
                barrier,
                inc=1,
                device_id={"row": row + dr, "col": col + dc},
                device_id_type=MESH,
            )

    own_in = [
        pltpu.make_async_copy(
            weight_in.at[l], win.at[l, pl.ds(dp * DH, DH), :], sem_local.at[l, 0]
        )
        for l in range(L)
    ]
    own_out = [
        pltpu.make_async_copy(
            weight_out.at[l],
            wout.at[l, :, :, pl.ds(dp * DH, DH)],
            sem_local.at[l, 1],
        )
        for l in range(L)
    ]
    for l in range(L):
        own_in[l].start()
        own_out[l].start()

    tall = H + 6
    zero_line = jnp.zeros((W + 2 * LEFT, LANES), F32)

    def clear(i, _):
        for j in range(J):
            for l in range(L):
                pads[l, j, i] = zero_line
            gpad[j, i] = zero_line
        return 0

    lax.fori_loop(0, tall, clear, 0)
    small[...] = jnp.zeros_like(small)
    for l in range(L):
        for p in range(7):
            for j in range(J):
                taps[l, j, 7 * p : 7 * p + 7, :] = kernel[
                    l, p, :, j * LANES : (j + 1) * LANES
                ]

    def fill(i, _):
        line = slides[0, i].astype(F32)
        for j in range(J):
            pads[0, j, i + 3, LEFT : LEFT + W, :] = line[:, j * LANES : (j + 1) * LANES]
        return 0

    lax.fori_loop(0, H, fill, 0)
    cor_wide[...] = jnp.zeros_like(cor_wide)

    def halo_copy(which, turn):
        if which < 4:
            dr, dc = STRAIGHT[which]
            if dr:
                src, dst = row_send.at[which], row_recv.at[turn, which]
            else:
                src, dst = col_send.at[which - 2], col_recv.at[turn, which - 2]
        else:
            dr, dc = DIAGONAL[which - 4]
            src, dst = cor_send.at[which - 4], cor_recv.at[turn, which - 4]
        where = {}
        if dr:
            where["row"] = row + dr
        if dc:
            where["col"] = col + dc
        return remote(src, dst, sem_hs.at[which], sem_hr.at[turn, which], **where)

    def lanes(j):
        return slice(j * LANES, (j + 1) * LANES)

    def halo_send(turn, src):
        for which, first in ((0, 3), (1, H)):
            for i in range(3):
                for j in range(J):
                    row_send[which, i, :, lanes(j)] = src[
                        j, first + i, LEFT : LEFT + W, :
                    ].astype(BF16)

            @pl.when(there(*STRAIGHT[which]))
            def _():
                halo_copy(which, turn).start()

        for which, first in ((2, LEFT), (3, LEFT + W - 3)):
            for i in range(3):
                for j in range(J):
                    col_send[which - 2, i, :, lanes(j)] = src[
                        j, 3 : 3 + H, first + i, :
                    ].astype(BF16)

            @pl.when(there(*STRAIGHT[which]))
            def _():
                halo_copy(which, turn).start()

        for k, (dr, dc) in enumerate(DIAGONAL):
            first, start = (3 if dr < 0 else H), (LEFT if dc < 0 else LEFT + W - 3)
            for i in range(3):
                for j in range(J):
                    cor_wide[3 * i : 3 * i + 3, lanes(j)] = src[
                        j, first + i, start : start + 3, :
                    ]
            cor_send[k] = cor_wide[...].astype(BF16)

            @pl.when(there(dr, dc))
            def _():
                halo_copy(4 + k, turn).start()

    def halo_recv(turn, dst):
        for which in (0, 1):
            first = H + 3 if which == 0 else 0
            dr, dc = STRAIGHT[which]

            @pl.when(there(-dr, -dc))
            def _():
                halo_copy(which, turn).wait_recv()
                for i in range(3):
                    line = row_recv[turn, which, i].astype(F32)
                    for j in range(J):
                        dst[j, first + i, LEFT : LEFT + W, :] = line[:, lanes(j)]

        for which in (2, 3):
            first = LEFT + W if which == 2 else LEFT - 3
            dr, dc = STRAIGHT[which]

            @pl.when(there(-dr, -dc))
            def _():
                halo_copy(which, turn).wait_recv()
                for i in range(3):
                    line = col_recv[turn, which - 2, i].astype(F32)
                    for j in range(J):
                        dst[j, 3 : 3 + H, first + i, :] = line[:, lanes(j)]

        for k, (dr, dc) in enumerate(DIAGONAL):
            first, start = (H + 3 if dr < 0 else 0), (LEFT + W if dc < 0 else LEFT - 3)

            @pl.when(there(-dr, -dc))
            def _():
                halo_copy(4 + k, turn).wait_recv()
                block = cor_recv[turn, k].astype(F32)
                for i in range(3):
                    for j in range(J):
                        dst[j, first + i, start : start + 3, :] = block[
                            3 * i : 3 * i + 3, lanes(j)
                        ]

        for which in range(8):
            dr, dc = (STRAIGHT + DIAGONAL)[which]

            @pl.when(there(dr, dc))
            def _():
                halo_copy(which, turn).wait_send()

    quarter = row % QUARTERS
    pieces = 2

    def held(which, l, p, side, q):
        if which == 0:
            rows = DH // QUARTERS // pieces
            return win.at[
                l, pl.ds(side * DH + (q * pieces + p) * rows, rows), :
            ]
        tiles = NT // QUARTERS // pieces
        return wout.at[
            l, pl.ds((q * pieces + p) * tiles, tiles), :, pl.ds(side * DH, DH)
        ]

    def own(which, l, p):
        if which == 0:
            rows = DH // QUARTERS // pieces
            return weight_in.at[l, pl.ds((quarter * pieces + p) * rows, rows), :]
        tiles = NT // QUARTERS // pieces
        return weight_out.at[l, pl.ds((quarter * pieces + p) * tiles, tiles)]

    other = 1 - dp

    def w_x(l, which, p):
        k = (l * 2 + which) * pieces + p
        return remote(
            own(which, l, p),
            held(which, l, p, dp, quarter),
            sem_ws.at[0, k],
            sem_wr.at[0, k],
            dp=1 - dp,
        )

    def w_hop(l, which, p, stage):
        k = (l * 2 + which) * pieces + p
        bit = 2 if stage == 1 else 1
        q = flip(quarter, 2) if stage == 3 else quarter
        part = held(which, l, p, other, q)
        return remote(
            part, part, sem_ws.at[stage, k], sem_wr.at[stage, k], row=flip(row, bit)
        )

    def weights_x(l, which):
        for p in range(pieces):
            w_x(l, which, p).start()

    def weights_forward(l, which):
        for p in range(pieces):
            w_x(l, which, p).wait()
            w_hop(l, which, p, 1).start()
            w_hop(l, which, p, 2).start()

    def weights_second(l, which):
        for p in range(pieces):
            w_hop(l, which, p, 1).wait()
            w_hop(l, which, p, 3).start()

    def weights_ready(l, which):
        for p in range(pieces):
            w_hop(l, which, p, 2).wait()
            w_hop(l, which, p, 3).wait()
        (own_in, own_out)[which][l].wait()

    def conv(src, l, mirrored, base, put):
        blocks = H // 8

        def one(index, _):
            j, start = index // blocks, (index % blocks) * 8
            totals = base(j, start)
            for q in range(7):
                for line in range(14):
                    window = src[
                        j, start + line, LEFT - 3 + q : LEFT - 3 + q + W, :
                    ]
                    for p in range(7):
                        i = line - p
                        if 0 <= i < 8:
                            k = 7 * p + q
                            k = 48 - k if mirrored else k
                            totals[i] = totals[i] + window * taps[l, j, k : k + 1, :]
            put(j, start, totals)
            return 0

        lax.fori_loop(0, J * blocks, one, 0)

    def tap_sums(l):
        for q in range(7):

            def lane_block(j, _):
                def block(index, totals):
                    start = index * 8
                    totals = list(totals)
                    for part in range(0, W, 8):
                        ups = [
                            gpad[j, start + 3 + i, LEFT + part : LEFT + part + 8, :]
                            for i in range(8)
                        ]
                        for line in range(14):
                            first = LEFT - 3 + part + q
                            window = pads[l, j, start + line, first : first + 8, :]
                            for p in range(7):
                                i = line - p
                                if 0 <= i < 8:
                                    totals[p] = totals[p] + window * ups[i]
                    return tuple(totals)

                zero = jnp.zeros((8, LANES), F32)
                totals = lax.fori_loop(0, H // 8, block, (zero,) * 7)
                for p in range(7):
                    put_small(
                        l, 7 * p + q, j, jnp.sum(totals[p], axis=0, keepdims=True)
                    )
                return 0

            lax.fori_loop(0, J, lane_block, 0)

    M = small.shape[3]

    def put_small(l, line, j, value):
        unit = (line // 8) * J + j
        small[
            l, unit // (CD * M), (unit // M) % CD, unit % M, line % 8 : line % 8 + 1, :
        ] = value

    def put_row(l, line, value):
        for j in range(J):
            put_small(l, line, j, value[:, lanes(j)])

    def forward(l, last):
        bias_line = kernel_bias[l : l + 1, :]

        for j in range(J):
            mixed_bias[j] = bias_line[:, lanes(j)]

        def base(j, start):
            del start
            bias = mixed_bias[j]
            return [jnp.broadcast_to(bias, (W, LANES)) for _ in range(8)]

        def put(j, start, totals):
            for i in range(8):
                mixed[j, start + i] = totals[i]

        conv(pads.at[l], l, False, base, put)
        gain, shift = norm_gain[l : l + 1, :], norm_bias[l : l + 1, :]

        def norm(i, _):
            lines = pl.ds(i * W, W)
            value = jnp.concatenate([mixed[j, i] for j in range(J)], axis=1)
            center = value - jnp.mean(value, -1, keepdims=True)
            scale = lax.rsqrt(jnp.mean(center * center, -1, keepdims=True) + EPSILON)
            out = center * scale
            normed[l, lines, :] = out
            rstd[l, lines, :] = scale
            normal[l, lines, :] = (out * gain + shift).astype(BF16)
            return 0

        lax.fori_loop(0, H, norm, 0)
        weights_second(l, 0)
        weights_ready(l, 0)

        def expand(t, _):
            cols = pl.ds(pl.multiple_of(t * T, T), T)
            hidden = jnp.dot(normal[l], win[l, :, cols], preferred_element_type=F32)
            hidden = hidden + bias_in[l : l + 1, cols]
            square = hidden * hidden
            tangent = jnp.tanh(hidden * (COEF + (COEF * CUBIC) * square))
            half = 0.5 * hidden
            both = 1.0 + tangent
            act[l, t] = (half * both).astype(BF16)
            slope[l, t] = 0.5 * both + half * (1.0 - tangent * tangent) * (
                COEF + (3.0 * COEF * CUBIC) * square
            )
            return 0

        lax.fori_loop(0, NT, expand, 0)
        weights_second(l, 1)
        weights_ready(l, 1)
        branch[l] = jnp.broadcast_to(bias_out[l : l + 1, :], (N, D))

        def project(t, _):
            branch[l] += jnp.dot(act[l, t], wout[l, t], preferred_element_type=F32)
            return 0

        lax.fori_loop(0, NT, project, 0)
        scales = layer_scale[l : l + 1, :]

        def finish(i, _):
            part = scales * branch[l, pl.ds(i * W, W), :]
            for j in range(J):
                old = pads[l, j, i + 3, LEFT : LEFT + W, :]
                new = (old + part[:, lanes(j)]).astype(BF16)
                if last:
                    output[0, i, :, lanes(j)] = new
                else:
                    pads[l + 1, j, i + 3, LEFT : LEFT + W, :] = new.astype(F32)
            return 0

        lax.fori_loop(0, H, finish, 0)

    bits = []
    bit = 2
    while bit < R:
        bits.append(bit)
        bit *= 2
    levels = []
    count = UN
    for b in bits:
        halve = count // 2 >= C
        levels.append((b, count, halve))
        count = count // 2 if halve else count
    left_units = count
    per_col = left_units // C
    nb = len(bits)
    S_CORE, S_DP, S_ROW, S_COL = 0, 1, 2, 2 + nb
    S_COLG = S_COL + C - 1
    S_ROWG = S_COLG + C - 1
    S_COREG = S_ROWG + nb

    def unit_base(level):
        start = 0
        for b, n, halve in levels[:level]:
            if halve:
                start = start + ((row // b) % 2) * (n // 2)
        return start

    def g_core(l, t):
        return remote(
            grads.at[l, t, 1 - core],
            from_core.at[l, t],
            sem_gs.at[t, S_CORE],
            sem_gr.at[l, t, S_CORE],
            row=flip(row, 1),
        )

    def g_dp(l, t):
        return remote(
            grads.at[l, t, core, 1 - dp],
            from_dp.at[l, t],
            sem_gs.at[t, S_DP],
            sem_gr.at[l, t, S_DP],
            dp=1 - dp,
        )

    row_slot = []
    at = 0
    for b, n, halve in levels:
        row_slot.append(at)
        at += n // 2 if halve else n

    def g_row(l, t, level):
        b, n, halve = levels[level]
        mine = (row // b) % 2
        start = unit_base(level)
        m = n
        if halve:
            m = n // 2
            start = start + (1 - mine) * m
        return remote(
            grads.at[l, t, core, dp, pl.ds(start, m)],
            from_row.at[l, t, pl.ds(row_slot[level], m)],
            sem_gs.at[t, S_ROW + level],
            sem_gr.at[l, t, S_ROW + level],
            row=flip(row, b),
        )

    def g_row_add(l, t, level):
        b, n, halve = levels[level]
        start = unit_base(level + 1)
        m = n // 2 if halve else n
        mine = grads.at[l, t, core, dp, pl.ds(start, m)]
        mine[...] = mine[...] + from_row[l, t, pl.ds(row_slot[level], m)]

    col_base = unit_base(nb)

    def g_col(l, t, k):
        peer = (col + k) % C
        return remote(
            grads.at[l, t, core, dp, pl.ds(col_base + peer * per_col, per_col)],
            from_col.at[l, t, k - 1],
            sem_gs.at[t, S_COL + k - 1],
            sem_gr.at[l, t, S_COL + k - 1],
            col=peer,
        )

    def g_colg(l, t, k):
        peer = (col + k) % C
        part = final.at[l, core, t, pl.ds(col_base + col * per_col, per_col)]
        return remote(
            part,
            part,
            sem_gs.at[t, S_COLG + k - 1],
            sem_gr.at[l, t, S_COLG + k - 1],
            col=peer,
        )

    def g_rowg(l, t, level):
        b, n, halve = levels[level]
        part = final.at[l, core, t, pl.ds(unit_base(level + 1), n // 2)]
        return remote(
            part,
            part,
            sem_gs.at[t, S_ROWG + level],
            sem_gr.at[l, t, S_ROWG + level],
            row=flip(row, b),
        )

    def g_coreg(l, t):
        part = final.at[l, core, t]
        return remote(
            part,
            part,
            sem_gs.at[t, S_COREG],
            sem_gr.at[l, t, S_COREG],
            row=flip(row, 1),
        )

    def go_dp(l, t):
        g_core(l, t).wait()
        mine = grads.at[l, t, core]
        mine[...] = mine[...] + from_core[l, t]
        g_dp(l, t).start()

    def go_row(l, t):
        g_dp(l, t).wait()
        mine = grads.at[l, t, core, dp]
        mine[...] = mine[...] + from_dp[l, t]
        for level in range(nb):
            if level:
                g_row(l, t, level - 1).wait()
                g_row_add(l, t, level - 1)
            g_row(l, t, level).start()

    def go_col(l, t):
        if nb:
            g_row(l, t, nb - 1).wait()
            g_row_add(l, t, nb - 1)
        for k in range(1, C):
            g_col(l, t, k).start()

    def go_colg(l, t):
        for k in range(1, C):
            g_col(l, t, k).wait()
        place = pl.ds(col_base + col * per_col, per_col)
        total = grads[l, t, core, dp, place].astype(F32)
        for k in range(1, C):
            total = total + from_col[l, t, k - 1].astype(F32)
        final[l, core, t, place] = total.astype(BF16)
        for k in range(1, C):
            g_colg(l, t, k).start()

    halved = [k for k in range(nb) if levels[k][2]][::-1]

    def go_rowg(l, t):
        for k in range(1, C):
            g_colg(l, t, k).wait()
        for n, level in enumerate(halved):
            if n:
                g_rowg(l, t, halved[n - 1]).wait()
            g_rowg(l, t, level).start()

    def go_coreg(l, t):
        if halved:
            g_rowg(l, t, halved[-1]).wait()
        g_coreg(l, t).start()

    def out_copies(l, t):
        cols = pl.ds(pl.multiple_of(t * T, T), T)
        return (
            pltpu.make_async_copy(
                final.at[l, 0, t], out_in.at[l, :, :, cols], sem_out.at[0, l, t]
            ),
            pltpu.make_async_copy(
                final.at[l, 1, t], out_out.at[l, t], sem_out.at[1, l, t]
            ),
        )

    def go_out(l, t):
        g_coreg(l, t).wait()
        for copy in out_copies(l, t):
            copy.start()

    chain = (go_row, go_col, go_colg, go_rowg, go_coreg, go_out)

    def tick(l, m):
        for behind, stage in enumerate(chain):
            t = m - behind
            if isinstance(m, int):
                if 0 <= t < NT:
                    stage(l, t)
            else:

                @pl.when(jnp.logical_and(t >= 0, t < NT))
                def _():
                    stage(l, t)

    ticks = NT + len(chain) - 1

    def run_ticks(l, first, end):
        def one(m, _):
            tick(l, m)
            return 0

        lax.fori_loop(first, end, one, 0)

    def s_copy(l, stage, k):
        if stage in (0, 3):
            peer = (row + k) % R
            where = {"row": peer}
        else:
            peer, pc, pd = cd_peer(k)
            where = {"col": pc, "dp": pd}
        if stage == 0:
            src, dst = small.at[l, peer], small_row.at[l, k - 1]
        elif stage == 1:
            src, dst = small.at[l, row, peer], small_cd.at[l, k - 1]
        elif stage == 2:
            src = dst = small_out.at[l, row, cd]
        else:
            src = dst = small_out.at[l, row]
        return remote(
            src, dst, sem_ss.at[stage, k - 1], sem_sr.at[l, stage, k - 1], **where
        )

    def small_start(l):
        for k in range(1, R):
            s_copy(l, 0, k).start()

    def small_second(l):
        for k in range(1, R):
            s_copy(l, 0, k).wait()
        total = small[l, row]
        for k in range(1, R):
            total = total + small_row[l, k - 1]
        small[l, row] = total
        for k in range(1, CD):
            s_copy(l, 1, k).start()

    def small_third(l):
        for k in range(1, CD):
            s_copy(l, 1, k).wait()
        total = small[l, row, cd]
        for k in range(1, CD):
            total = total + small_cd[l, k - 1]
        small_out[l, row, cd] = total
        for k in range(1, CD):
            s_copy(l, 2, k).start()

    def small_fourth(l):
        for k in range(1, CD):
            s_copy(l, 2, k).wait()
        for k in range(1, R):
            s_copy(l, 3, k).start()

    def small_end(l):
        for k in range(1, R):
            s_copy(l, 3, k).wait()

    def backward(l, turn, busy, last):
        scales = layer_scale[l : l + 1, :]
        empty = jnp.zeros((8, D), F32)

        def fold(value):
            total = value[0:8]
            for k in range(8, value.shape[0], 8):
                total = total + value[k : k + 8]
            return total

        def before(i, sums):
            lines = pl.ds(i * W, W)
            up = upstream[lines, :]
            gb = up * scales
            gb_low[lines, :] = gb.astype(BF16)
            return (sums[0] + fold(up * branch[l, lines, :]), sums[1] + fold(gb))

        sums = lax.fori_loop(0, H, before, (empty,) * 2)
        put_row(l, 53, jnp.sum(sums[0], 0, keepdims=True))
        put_row(l, 52, jnp.sum(sums[1], 0, keepdims=True))
        gnorm[...] = jnp.zeros_like(gnorm)

        def tile(t, _):
            cols = pl.ds(pl.multiple_of(t * T, T), T)
            gb = gb_low[...]
            ga = lax.dot_general(gb, wout[l, t], COLS, preferred_element_type=F32)
            gh = ga * slope[l, t]
            gbias[t] = jnp.sum(gh, 0, keepdims=True)
            low = gh.astype(BF16)
            g_out = lax.dot_general(act[l, t], gb, ROWS, preferred_element_type=F32)
            g_in = lax.dot_general(normal[l], low, ROWS, preferred_element_type=F32)
            for d in range(DP):
                grads[l, t, 0, d] = (
                    g_in[d * DH : (d + 1) * DH].astype(BF16).reshape(UN, UNIT, T)
                )
                grads[l, t, 1, d] = (
                    g_out[:, d * DH : (d + 1) * DH].astype(BF16).reshape(UN, UNIT, T)
                )
            g_core(l, t).start()
            gnorm[...] += lax.dot_general(
                low, win[l, :, cols], COLS, preferred_element_type=F32
            )

            @pl.when(t >= 2)
            def _():
                go_dp(l, t - 2)

            busy(t)
            return 0

        lax.fori_loop(0, NT, tile, 0)
        for t in range(NT - 2, NT):
            go_dp(l, t)
        per_line = D // T
        for t in range(NT):
            for half in range(T // LANES):
                j = (t % per_line) * (T // LANES) + half
                put_small(l, 54 + t // per_line, j, gbias[t, :, lanes(half)])
        gain = norm_gain[l : l + 1, :]

        def after(i, sums):
            lines = pl.ds(i * W, W)
            gn, unit = gnorm[lines, :], normed[l, lines, :]
            both = gn * unit
            gs = gn * gain
            first = jnp.mean(gs, -1, keepdims=True)
            second = jnp.mean(gs * unit, -1, keepdims=True)
            gm = rstd[l, lines, :] * (gs - first - unit * second)
            for j in range(J):
                gpad[j, i + 3, LEFT : LEFT + W, :] = gm[:, lanes(j)]
            return (sums[0] + fold(gm), sums[1] + fold(both), sums[2] + fold(gn))

        sums = lax.fori_loop(0, H, after, (empty,) * 3)
        for k in range(3):
            put_row(l, 49 + k, jnp.sum(sums[k], 0, keepdims=True))
        halo_send(turn, gpad)
        tap_sums(l)
        small_start(l)
        halo_recv(turn, gpad)

        def base(j, start):
            return [up_block[j, start + i] for i in range(8)]

        up_block = mixed

        def spread(i, _):
            for j in range(J):
                mixed[j, i] = upstream[pl.ds(i * W, W), lanes(j)]
            return 0

        lax.fori_loop(0, H, spread, 0)

        def put(j, start, totals):
            for i in range(8):
                mixed[j, start + i] = totals[i]

        small_second(l)
        conv(gpad, l, True, base, put)

        def gather(i, _):
            for j in range(J):
                if last:
                    grad_slides[0, i, :, lanes(j)] = mixed[j, i].astype(BF16)
                else:
                    upstream[pl.ds(i * W, W), lanes(j)] = mixed[j, i]
            return 0

        lax.fori_loop(0, H, gather, 0)

    diagonals = jnp.where(row > 0, 1, 0) + jnp.where(row < R - 1, 1, 0)
    diagonals = diagonals * (
        jnp.where(col > 0, 1, 0) + jnp.where(col < C - 1, 1, 0)
    )
    pl.semaphore_wait(barrier, R - 1 + CD - 1 + diagonals)
    halo_send(0, pads.at[0])
    for l in range(L):
        for which in range(2):
            weights_x(l, which)
    halo_recv(0, pads.at[0])

    def start_up(i, _):
        upstream[pl.ds(i * W, W), :] = cotangent[0, i].astype(F32)
        return 0

    lax.fori_loop(0, H, start_up, 0)
    weights_forward(0, 0)
    for l in range(L):
        if l:
            halo_recv(l, pads.at[l])
            weights_forward(l, 0)
        weights_forward(l, 1)
        forward(l, l == L - 1)
        if l + 1 < L:
            halo_send(l + 1, pads.at[l + 1])

    done = 0
    for n, l in enumerate(reversed(range(L))):
        if n == 0:
            backward(l, L + n, lambda t: None, l == 0)
        else:
            prior = l + 1

            def busy(t, prior=prior):
                @pl.when(t % 3 == 2)
                def _():
                    tick(prior, 1 + t // 3)

            run_ticks(prior, 0, 1)
            small_third(prior)
            backward(l, L + n, busy, l == 0)
            small_fourth(prior)
            done = 1 + NT // 3
            run_ticks(prior, done, ticks)
            small_end(prior)
    small_third(0)
    small_fourth(0)
    run_ticks(0, 0, ticks)
    small_end(0)
    for l in range(L):
        pltpu.sync_copy(small_out.at[l], out_small.at[l])

    def drain(t, _):
        for l in range(L):
            for copy in out_copies(l, t):
                copy.wait()
        return 0

    lax.fori_loop(0, NT, drain, 0)


def per_device(
    sizes,
    slides,
    cotangent,
    kernel,
    kernel_bias,
    norm_gain,
    norm_bias,
    weight_in,
    bias_in,
    weight_out,
    bias_out,
    layer_scale,
):
    R, C, DP = sizes["row"], sizes["col"], sizes["dp"]
    CD = C * DP
    L, DH, FF = weight_in.shape
    D = slides.shape[-1]
    H, W = slides.shape[1], slides.shape[2]
    N = H * W
    J = D // LANES
    T = DH
    NT = FF // T
    UN = DH // UNIT
    everyone = R * CD
    need = -(-(54 + FF // D) // 8) * J
    M = -(-need // everyone)
    row_units, count, bit, nb = 0, UN, 2, 0
    while bit < R:
        halve = count // 2 >= C
        count = count // 2 if halve else count
        row_units += count
        bit *= 2
        nb += 1
    per_col = count // C
    stages = 2 + nb + 2 * (C - 1) + nb + 1
    small_peers = max(R, CD) - 1
    vmem = pl.BlockSpec(memory_space=pltpu.VMEM)
    hbm = pl.BlockSpec(memory_space=pl.ANY)
    V = pltpu.VMEM
    DMA = pltpu.SemaphoreType.DMA
    turns = 2 * L
    out = pl.pallas_call(
        functools.partial(step_body, sizes),
        out_shape=(
            jax.ShapeDtypeStruct((1, H, W, D), BF16),
            jax.ShapeDtypeStruct((1, H, W, D), BF16),
            jax.ShapeDtypeStruct((L, UN, UNIT, FF), BF16),
            jax.ShapeDtypeStruct((L, NT, UN, UNIT, DH), BF16),
            jax.ShapeDtypeStruct((L, R, CD, M, 8, LANES), F32),
        ),
        in_specs=[vmem] * 6 + [hbm, vmem, hbm, vmem, vmem],
        out_specs=(vmem, vmem, hbm, hbm, hbm),
        scratch_shapes=[
            V((L, J, H + 6, W + 2 * LEFT, LANES), F32),
            V((J, H + 6, W + 2 * LEFT, LANES), F32),
            V((L, J, 49, LANES), F32),
            V((J, H, W, LANES), F32),
            V((L, D, FF), BF16),
            V((L, NT, T, D), BF16),
            V((L, N, D), F32),
            V((L, N, 1), F32),
            V((L, N, D), BF16),
            V((L, NT, N, T), BF16),
            V((L, NT, N, T), F32),
            V((L, N, D), F32),
            V((N, D), F32),
            V((N, D), BF16),
            V((N, D), F32),
            V((NT, 1, T), F32),
            V((J, 1, LANES), F32),
            V((L, NT, 2, DP, UN, UNIT, T), BF16),
            V((L, NT, DP, UN, UNIT, T), BF16),
            V((L, NT, UN, UNIT, T), BF16),
            V((L, NT, max(row_units, 1), UNIT, T), BF16),
            V((L, NT, max(C - 1, 1), per_col, UNIT, T), BF16),
            V((L, 2, NT, UN, UNIT, T), BF16),
            V((L, R, CD, M, 8, LANES), F32),
            V((L, max(R - 1, 1), CD, M, 8, LANES), F32),
            V((L, max(CD - 1, 1), M, 8, LANES), F32),
            V((L, R, CD, M, 8, LANES), F32),
            V((2, 3, W, D), BF16),
            V((2, 3, H, D), BF16),
            V((4, UNIT, D), BF16),
            V((turns, 2, 3, W, D), BF16),
            V((turns, 2, 3, H, D), BF16),
            V((turns, 4, UNIT, D), BF16),
            V((UNIT, D), F32),
            DMA((L, 2)),
            DMA((4, 4 * L)),
            DMA((4, 4 * L)),
            DMA((8,)),
            DMA((turns, 8)),
            DMA((NT, stages)),
            DMA((L, NT, stages)),
            DMA((4, small_peers)),
            DMA((L, 4, small_peers)),
            DMA((2, L, NT)),
        ],
        compiler_params=pltpu.CompilerParams(
            collective_id=0, has_side_effects=True, vmem_limit_bytes=67043328
        ),
        name="step",
    )(
        slides,
        cotangent,
        kernel,
        kernel_bias,
        norm_gain,
        norm_bias,
        weight_in,
        bias_in,
        weight_out.reshape(L, NT, T, DH),
        bias_out,
        layer_scale,
    )
    output, grad_slides, low_in, low_out, small = out
    lines = small.reshape(L, -1, J, 8, LANES).transpose(0, 1, 3, 2, 4)
    lines = lines.reshape(L, -1, D)
    return (
        output,
        grad_slides,
        low_in.reshape(L, DH, FF).astype(F32),
        low_out.reshape(L, FF, DH).astype(F32),
        lines[:, :49].reshape(L, 7, 7, D),
        lines[:, 49:54],
        lines[:, 54 : 54 + FF // D].reshape(L, FF),
    )


def solution(mesh):
    return jax.shard_map(
        functools.partial(per_device, dict(mesh.shape)),
        mesh=mesh,
        in_specs=(
            P("dp", "row", "col", None),
            P("dp", "row", "col", None),
            P(),
            P(),
            P(),
            P(),
            P(None, "dp", None),
            P(),
            P(None, None, "dp"),
            P(),
            P(),
        ),
        out_specs=(
            P("dp", "row", "col", None),
            P("dp", "row", "col", None),
            P(None, "dp", None),
            P(None, None, "dp"),
            P(),
            P(),
            P(),
        ),
        check_vma=False,
    )
```

profile of v0, /device:TPU:0, one launch (start us, length us, event | category | flops | bytes accessed | tf_op | source)
XLA Modules:
  0.0 207.8 jit_solution(13983157097128153062)
XLA Ops:
  0.6 1.7 copy.18.kernel
  2.3 194.0 %step.1 = (bf16[1,16,32,512]{3,2,1,0:T(8,128)(2,1)}, bf16[1,16,32,512]{3,2,1,0:T(8,128)(2,1)}, bf16[2,16,16,2048]{3,2,1,0:T(8,128)(2,1)}, bf16[2,8,16,16,256]{4,3,2,1,0:T(8,128)(2,1)}, f32[2,4,8,1,8,128]{5,4,3,2,1,0:T(8,128)}) custom-call(bf16[1,16,32,512]{3,2,1,0:T(8,128)(2,1)} %slides.1, bf16[1,16,32,512]{3,2,1,0:T(8,128)(2,1)} %cotangent.1, ...), custom_call_target="tpu_custom_call" | custom-call | tf_op jit(solution)/shard_map/step/pallas_call | solution.py:965
  196.3 1.0 copy.19
  197.4 0.2 reshape.37
  197.6 0.6 slice.14
  198.2 0.6 slice.13
  198.8 0.7 slice.12
  199.5 0.0 copy-start
  199.5 4.3 %bitcast_convert_fusion.1 = f32[2,256,2048]{2,1,0:T(8,128)} fusion(bf16[2,16,16,2048]{3,2,1,0:T(8,128)(2,1)} %get-tuple-element.14), kind=kLoop, calls=%fused_computation.1 | loop fusion | flops 1048576 | bytes 6291456 | tf_op jit(solution)/shard_map/convert_element_type | solution.py:1045
  203.8 0.0 copy-done
  203.8 0.0 copy-start.2
  203.8 0.0 copy-start.1
  203.8 2.5 %bitcast_convert_fusion = f32[2,2048,256]{2,1,0:T(8,128)} fusion(bf16[2,8,16,16,256]{4,3,2,1,0:T(8,128)(2,1)S(1)} %copy-done), kind=kLoop, calls=%fused_computation | loop fusion | flops 1048576 | bytes 6291456 | tf_op jit(solution)/shard_map/convert_element_type | solution.py:1046
  206.2 0.0 copy-done.2
  206.3 0.8 copy.22
  207.0 0.0 copy-done.1
  207.0 0.8 copy.23
Async XLA Ops:
  199.5 4.3 %copy-start = (bf16[2,8,16,16,256]{4,3,2,1,0:T(8,128)(2,1)S(1)}, bf16[2,8,16,16,256]{4,3,2,1,0:T(8,128)(2,1)}, u32[]{:S(2)}) copy-start(bf16[2,8,16,16,256]{4,3,2,1,0:T(8,128)(2,1)} %get-tuple-element.15) | copy-start | bytes 6291460
  203.8 2.5 %copy-start.2 = (bf16[1,16,32,512]{3,2,1,0:T(8,128)(2,1)S(1)}, bf16[1,16,32,512]{3,2,1,0:T(8,128)(2,1)}, u32[]{:S(2)}) copy-start(bf16[1,16,32,512]{3,2,1,0:T(8,128)(2,1)} %get-tuple-element.24) | copy-start | bytes 1572868
  203.8 3.3 %copy-start.1 = (bf16[1,16,32,512]{3,2,1,0:T(8,128)(2,1)S(1)}, bf16[1,16,32,512]{3,2,1,0:T(8,128)(2,1)}, u32[]{:S(2)}) copy-start(bf16[1,16,32,512]{3,2,1,0:T(8,128)(2,1)} %get-tuple-element.25) | copy-start | bytes 1572868
where the time goes:
time: 208 us
  Pallas kernels  194 us (93%)
  other arithmetic  6.76 us (3%)
  local copies, waits for them, and re-layouts  6.39 us (3%)
    pallas_call x1, Pallas kernels, per_device(): pl.pallas_call(functools.partial(step_body, sizes), out_shape=(jax.ShapeD...  194 us
    convert_element_type x1, other arithmetic, per_device(): low_in.reshape(L, DH, FF).astype(F32)  4.28 us

commit v1 on v0

--- a/solution.py
+++ b/solution.py
@@ -19,7 +19,6 @@
 BF16 = jnp.bfloat16
 STRAIGHT = ((-1, 0), (1, 0), (0, -1), (0, 1))
 DIAGONAL = ((-1, -1), (-1, 1), (1, -1), (1, 1))
-ROWS = (((0,), (0,)), ((), ()))
 COLS = (((1,), (1,)), ((), ()))
 
 
@@ -42,7 +41,7 @@
     out_out,
     out_small,
     pads,
-    gpad,
+    gpads,
     taps,
     mixed,
     win,
@@ -50,11 +49,13 @@
     normed,
     rstd,
     normal,
+    normal_t,
     act,
     slope,
     branch,
     upstream,
     gb_low,
+    gb_t,
     gnorm,
     gbias,
     mixed_bias,
@@ -170,7 +171,7 @@
         for j in range(J):
             for l in range(L):
                 pads[l, j, i] = zero_line
-            gpad[j, i] = zero_line
+                gpads[l, j, i] = zero_line
         return 0
 
     lax.fori_loop(0, tall, clear, 0)
@@ -178,9 +179,10 @@
     for l in range(L):
         for p in range(7):
             for j in range(J):
-                taps[l, j, 7 * p : 7 * p + 7, :] = kernel[
-                    l, p, :, j * LANES : (j + 1) * LANES
-                ]
+                for q in range(7):
+                    taps[l, j, 7 * p + q : 7 * p + q + 1, :] = kernel[
+                        p, q, l : l + 1, j * LANES : (j + 1) * LANES
+                    ]
 
     def fill(i, _):
         line = slides[0, i].astype(F32)
@@ -293,25 +295,20 @@
                 halo_copy(which, turn).wait_send()
 
     quarter = row % QUARTERS
-    pieces = 2
+    pieces = NT // QUARTERS
 
     def held(which, l, p, side, q):
+        t = q * pieces + p
         if which == 0:
-            rows = DH // QUARTERS // pieces
-            return win.at[
-                l, pl.ds(side * DH + (q * pieces + p) * rows, rows), :
-            ]
-        tiles = NT // QUARTERS // pieces
-        return wout.at[
-            l, pl.ds((q * pieces + p) * tiles, tiles), :, pl.ds(side * DH, DH)
-        ]
+            cols = pl.ds(pl.multiple_of(t * T, T), T)
+            return win.at[l, pl.ds(side * DH, DH), cols]
+        return wout.at[l, t, :, pl.ds(side * DH, DH)]
 
     def own(which, l, p):
+        t = quarter * pieces + p
         if which == 0:
-            rows = DH // QUARTERS // pieces
-            return weight_in.at[l, pl.ds((quarter * pieces + p) * rows, rows), :]
-        tiles = NT // QUARTERS // pieces
-        return weight_out.at[l, pl.ds((quarter * pieces + p) * tiles, tiles)]
+            return weight_in.at[l, :, pl.ds(pl.multiple_of(t * T, T), T)]
+        return weight_out.at[l, t]
 
     other = 1 - dp
 
@@ -338,24 +335,24 @@
         for p in range(pieces):
             w_x(l, which, p).start()
 
-    def weights_forward(l, which):
-        for p in range(pieces):
-            w_x(l, which, p).wait()
-            w_hop(l, which, p, 1).start()
-            w_hop(l, which, p, 2).start()
-
-    def weights_second(l, which):
-        for p in range(pieces):
-            w_hop(l, which, p, 1).wait()
-            w_hop(l, which, p, 3).start()
-
-    def weights_ready(l, which):
-        for p in range(pieces):
-            w_hop(l, which, p, 2).wait()
-            w_hop(l, which, p, 3).wait()
-        (own_in, own_out)[which][l].wait()
-
-    def conv(src, l, mirrored, base, put):
+    def weights_forward(l, which, p):
+        w_x(l, which, p).wait()
+        w_hop(l, which, p, 1).start()
+        w_hop(l, which, p, 2).start()
+
+    def weights_second(l, which, p):
+        w_hop(l, which, p, 1).wait()
+        w_hop(l, which, p, 3).start()
+
+    def weights_got(l, which, p, stage):
+        w_hop(l, which, p, stage).wait()
+
+    def my_tile(s):
+        q, p = s // pieces, s % pieces
+        spot = flip(quarter, 1) * (q % 2) + quarter * (1 - q % 2)
+        return ((spot + 2 * (q // 2)) % QUARTERS) * pieces + p
+
+    def conv(src, l, mirrored, base, put, during=None):
         blocks = H // 8
 
         def one(index, _):
@@ -373,12 +370,14 @@
                             k = 48 - k if mirrored else k
                             totals[i] = totals[i] + window * taps[l, j, k : k + 1, :]
             put(j, start, totals)
+            if during is not None:
+                during(index)
             return 0
 
         lax.fori_loop(0, J * blocks, one, 0)
 
-    def tap_sums(l):
-        for q in range(7):
+    def tap_sums(l, first, end, during):
+        for q in range(first, end):
 
             def lane_block(j, _):
                 def block(index, totals):
@@ -386,7 +385,9 @@
                     totals = list(totals)
                     for part in range(0, W, 8):
                         ups = [
-                            gpad[j, start + 3 + i, LEFT + part : LEFT + part + 8, :]
+                            gpads[
+                                l, j, start + 3 + i, LEFT + part : LEFT + part + 8, :
+                            ]
                             for i in range(8)
                         ]
                         for line in range(14):
@@ -407,6 +408,7 @@
                 return 0
 
             lax.fori_loop(0, J, lane_block, 0)
+            during(q)
 
     M = small.shape[3]
 
@@ -420,9 +422,13 @@
         for j in range(J):
             put_small(l, line, j, value[:, lanes(j)])
 
-    def forward(l, last):
+    def transpose(src, dst):
+        for k in range(N // LANES):
+            block = src[k * LANES : (k + 1) * LANES, :].astype(F32)
+            dst[:, lanes(k)] = block.T.astype(BF16)
+
+    def forward(l, last, hooks):
         bias_line = kernel_bias[l : l + 1, :]
-
         for j in range(J):
             mixed_bias[j] = bias_line[:, lanes(j)]
 
@@ -435,7 +441,8 @@
             for i in range(8):
                 mixed[j, start + i] = totals[i]
 
-        conv(pads.at[l], l, False, base, put)
+        conv(pads.at[l], l, False, base, put, hooks["conv"])
+        hooks["conv"](-1)
         gain, shift = norm_gain[l : l + 1, :], norm_bias[l : l + 1, :]
 
         def norm(i, _):
@@ -449,11 +456,13 @@
             normal[l, lines, :] = (out * gain + shift).astype(BF16)
             return 0
 
-        lax.fori_loop(0, H, norm, 0)
-        weights_second(l, 0)
-        weights_ready(l, 0)
-
-        def expand(t, _):
+        lax.fori_loop(0, H, norm, 0, unroll=4)
+        hooks["norm"]()
+        transpose(normal.at[l], normal_t.at[l])
+
+        def expand(s, _):
+            hooks["expand"](s)
+            t = my_tile(s)
             cols = pl.ds(pl.multiple_of(t * T, T), T)
             hidden = jnp.dot(normal[l], win[l, :, cols], preferred_element_type=F32)
             hidden = hidden + bias_in[l : l + 1, cols]
@@ -462,21 +471,27 @@
             half = 0.5 * hidden
             both = 1.0 + tangent
             act[l, t] = (half * both).astype(BF16)
-            slope[l, t] = 0.5 * both + half * (1.0 - tangent * tangent) * (
+            rise = 0.5 * both + half * (1.0 - tangent * tangent) * (
                 COEF + (3.0 * COEF * CUBIC) * square
             )
+            slope[l, t] = rise.astype(BF16)
             return 0
 
         lax.fori_loop(0, NT, expand, 0)
-        weights_second(l, 1)
-        weights_ready(l, 1)
         branch[l] = jnp.broadcast_to(bias_out[l : l + 1, :], (N, D))
 
-        def project(t, _):
-            branch[l] += jnp.dot(act[l, t], wout[l, t], preferred_element_type=F32)
+        def project(s, _):
+            hooks["project"](s)
+            total = branch[l]
+            for p in range(pieces):
+                t = my_tile(s * pieces + p)
+                total = total + jnp.dot(
+                    act[l, t], wout[l, t], preferred_element_type=F32
+                )
+            branch[l] = total
             return 0
 
-        lax.fori_loop(0, NT, project, 0)
+        lax.fori_loop(0, QUARTERS, project, 0)
         scales = layer_scale[l : l + 1, :]
 
         def finish(i, _):
@@ -665,7 +680,7 @@
                 final.at[l, 0, t], out_in.at[l, :, :, cols], sem_out.at[0, l, t]
             ),
             pltpu.make_async_copy(
-                final.at[l, 1, t], out_out.at[l, t], sem_out.at[1, l, t]
+                final.at[l, 1, t], out_out.at[l, :, :, cols], sem_out.at[1, l, t]
             ),
         )
 
@@ -675,27 +690,6 @@
             copy.start()
 
     chain = (go_row, go_col, go_colg, go_rowg, go_coreg, go_out)
-
-    def tick(l, m):
-        for behind, stage in enumerate(chain):
-            t = m - behind
-            if isinstance(m, int):
-                if 0 <= t < NT:
-                    stage(l, t)
-            else:
-
-                @pl.when(jnp.logical_and(t >= 0, t < NT))
-                def _():
-                    stage(l, t)
-
-    ticks = NT + len(chain) - 1
-
-    def run_ticks(l, first, end):
-        def one(m, _):
-            tick(l, m)
-            return 0
-
-        lax.fori_loop(first, end, one, 0)
 
     def s_copy(l, stage, k):
         if stage in (0, 3):
@@ -750,7 +744,8 @@
         for k in range(1, R):
             s_copy(l, 3, k).wait()
 
-    def backward(l, turn, busy, last):
+    def backward(l, turn, hooks, last):
+        gpad = gpads.at[l]
         scales = layer_scale[l : l + 1, :]
         empty = jnp.zeros((8, D), F32)
 
@@ -771,22 +766,23 @@
         put_row(l, 53, jnp.sum(sums[0], 0, keepdims=True))
         put_row(l, 52, jnp.sum(sums[1], 0, keepdims=True))
         gnorm[...] = jnp.zeros_like(gnorm)
+        transpose(gb_low, gb_t)
 
         def tile(t, _):
             cols = pl.ds(pl.multiple_of(t * T, T), T)
             gb = gb_low[...]
             ga = lax.dot_general(gb, wout[l, t], COLS, preferred_element_type=F32)
-            gh = ga * slope[l, t]
+            gh = ga * slope[l, t].astype(F32)
             gbias[t] = jnp.sum(gh, 0, keepdims=True)
             low = gh.astype(BF16)
-            g_out = lax.dot_general(act[l, t], gb, ROWS, preferred_element_type=F32)
-            g_in = lax.dot_general(normal[l], low, ROWS, preferred_element_type=F32)
+            g_out = jnp.dot(gb_t[...], act[l, t], preferred_element_type=F32)
+            g_in = jnp.dot(normal_t[l], low, preferred_element_type=F32)
             for d in range(DP):
                 grads[l, t, 0, d] = (
                     g_in[d * DH : (d + 1) * DH].astype(BF16).reshape(UN, UNIT, T)
                 )
                 grads[l, t, 1, d] = (
-                    g_out[:, d * DH : (d + 1) * DH].astype(BF16).reshape(UN, UNIT, T)
+                    g_out[d * DH : (d + 1) * DH].astype(BF16).reshape(UN, UNIT, T)
                 )
             g_core(l, t).start()
             gnorm[...] += lax.dot_general(
@@ -797,12 +793,13 @@
             def _():
                 go_dp(l, t - 2)
 
-            busy(t)
+            hooks('tile', t)
             return 0
 
         lax.fori_loop(0, NT, tile, 0)
         for t in range(NT - 2, NT):
             go_dp(l, t)
+        hooks('rest', -1)
         per_line = D // T
         for t in range(NT):
             for half in range(T // LANES):
@@ -822,12 +819,11 @@
                 gpad[j, i + 3, LEFT : LEFT + W, :] = gm[:, lanes(j)]
             return (sums[0] + fold(gm), sums[1] + fold(both), sums[2] + fold(gn))
 
-        sums = lax.fori_loop(0, H, after, (empty,) * 3)
+        sums = lax.fori_loop(0, H, after, (empty,) * 3, unroll=2)
         for k in range(3):
             put_row(l, 49 + k, jnp.sum(sums[k], 0, keepdims=True))
         halo_send(turn, gpad)
-        tap_sums(l)
-        small_start(l)
+        hooks('sent', -1)
         halo_recv(turn, gpad)
 
         def base(j, start):
@@ -846,8 +842,7 @@
             for i in range(8):
                 mixed[j, start + i] = totals[i]
 
-        small_second(l)
-        conv(gpad, l, True, base, put)
+        conv(gpad, l, True, base, put, lambda k: hooks('conv', k))
 
         def gather(i, _):
             for j in range(J):
@@ -875,39 +870,173 @@
         return 0
 
     lax.fori_loop(0, H, start_up, 0)
-    weights_forward(0, 0)
+
+    def at(value, index, call):
+        @pl.when(value == index)
+        def _():
+            call()
+
+    blocks = J * (H // 8)
+    spread_out = [(k, max(blocks * (2 * k + 1) // (2 * pieces), 1)) for k in range(pieces)]
+
+    def first_conv(index):
+        if not isinstance(index, int):
+            for p, place in spread_out:
+                at(index, place, lambda: weights_forward(0, 0, p))
+
+    def first_norm():
+        weights_got(0, 0, 0, 2)
+        own_in[0].wait()
+
+    def first_expand(s):
+        def second(p):
+            weights_second(0, 0, p)
+
+        for p in range(pieces):
+            if p:
+                at(s, pieces + p, lambda: weights_got(0, 0, p, 2))
+            at(s, 2 * pieces - 1 + p, lambda: second(p))
+            at(s, 3 * pieces + p, lambda: weights_got(0, 0, p, 3))
+            at(s, (2 * p + 1) * pieces, lambda: weights_forward(0, 1, p))
+
+    def first_project(s):
+        def one():
+            for p in range(pieces):
+                weights_got(0, 1, p, 2)
+
+        def two():
+            for p in range(pieces):
+                weights_second(0, 1, p)
+
+        def three():
+            for p in range(pieces):
+                weights_got(0, 1, p, 3)
+
+        at(s, 0, lambda: own_out[0].wait())
+        at(s, 1, one)
+        at(s, 2, two)
+        at(s, 3, three)
+
+    def later(l):
+        def in_conv(index):
+            if isinstance(index, int):
+                for p in range(pieces):
+                    weights_second(l, 0, p)
+
+        def in_norm():
+            for p in range(pieces):
+                weights_got(l, 0, p, 2)
+                weights_got(l, 0, p, 3)
+            own_in[l].wait()
+
+        def in_expand(s):
+            for p in range(pieces):
+                at(s, NT // 2 + p, lambda: weights_second(l, 1, p))
+
+        def in_project(s):
+            def one():
+                for p in range(pieces):
+                    weights_got(l, 1, p, 2)
+                own_out[l].wait()
+
+            def three():
+                for p in range(pieces):
+                    weights_got(l, 1, p, 3)
+
+            at(s, 0, one)
+            at(s, 3, three)
+
+        return dict(conv=in_conv, norm=in_norm, expand=in_expand, project=in_project)
+
+    first = dict(
+        conv=first_conv, norm=first_norm, expand=first_expand, project=first_project
+    )
     for l in range(L):
         if l:
+            for which in range(2):
+                for p in range(pieces):
+                    weights_forward(l, which, p)
             halo_recv(l, pads.at[l])
-            weights_forward(l, 0)
-        weights_forward(l, 1)
-        forward(l, l == L - 1)
+        forward(l, l == L - 1, later(l) if l else first)
         if l + 1 < L:
             halo_send(l + 1, pads.at[l + 1])
 
-    done = 0
+    clock = [0.0]
+    due = []
+    link = [0.0]
+
+    def push(ready, chain, place, arg):
+        due.append((ready, len(due), chain, place, arg))
+
+    gchain = [
+        (go_row, 4.0),
+        (go_col, 4.0),
+        (go_colg, 4.0),
+        (go_rowg, 4.0),
+        (go_coreg, 2.0),
+        (go_out, 0.0),
+    ]
+    schain = [(small_second, 3.5), (small_third, 3.5), (small_fourth, 3.5), (small_end, 0)]
+
+    def run_due(now):
+        while due:
+            best = min(due)
+            if best[0] > now:
+                return
+            due.remove(best)
+            ready, _, chain, place, arg = best
+            chain[place][0](*arg)
+            if place + 1 < len(chain):
+                wait = chain[place][1]
+                push(max(ready, clock[0]) + wait, chain, place + 1, arg)
+
+    def spend(time):
+        clock[0] += time
+        run_due(clock[0])
+
+    TILE, CONV, TAP = 1.0, 0.55, 0.75
+    cut = 4
     for n, l in enumerate(reversed(range(L))):
-        if n == 0:
-            backward(l, L + n, lambda t: None, l == 0)
-        else:
-            prior = l + 1
-
-            def busy(t, prior=prior):
-                @pl.when(t % 3 == 2)
-                def _():
-                    tick(prior, 1 + t // 3)
-
-            run_ticks(prior, 0, 1)
-            small_third(prior)
-            backward(l, L + n, busy, l == 0)
-            small_fourth(prior)
-            done = 1 + NT // 3
-            run_ticks(prior, done, ticks)
-            small_end(prior)
-    small_third(0)
-    small_fourth(0)
-    run_ticks(0, 0, ticks)
-    small_end(0)
+        last = l == 0
+
+        def hooks(name, index, l=l, last=last):
+            if name == 'tile':
+                start = clock[0]
+                for t in range(NT):
+                    clock[0] = start + (t + 1) * TILE
+                    ready_now = [x for x in due if x[0] <= clock[0]]
+                    if ready_now:
+                        at(index, t, lambda: run_due(clock[0]))
+                for t in range(NT):
+                    begin = max(link[0], start + TILE * min(t + 3, NT))
+                    link[0] = begin + 2.75
+                    push(link[0] + 2.3, gchain, 0, (l, t))
+            elif name == 'rest':
+                spend(0.8)
+            elif name == 'sent':
+                spend(1.4)
+                if last:
+                    for k in range(1, L):
+                        tap_sums(k, cut, 7, lambda q: spend(TAP))
+                        small_start(k)
+                        push(clock[0] + 3.5, schain, 0, (k,))
+                    tap_sums(l, 0, 7, lambda q: spend(TAP))
+                    small_start(l)
+                    push(clock[0] + 3.5, schain, 0, (l,))
+                else:
+                    tap_sums(l, 0, cut, lambda q: spend(TAP))
+            elif name == 'conv':
+                start = clock[0]
+                for k in range(blocks):
+                    clock[0] = start + (k + 1) * CONV
+                    if [x for x in due if x[0] <= clock[0]]:
+                        at(index, k, lambda: run_due(clock[0]))
+
+        backward(l, L + n, hooks, last)
+        spend(0.8)
+    while due:
+        clock[0] = max(clock[0], min(due)[0])
+        run_due(clock[0])
     for l in range(L):
         pltpu.sync_copy(small_out.at[l], out_small.at[l])
 
@@ -968,14 +1097,14 @@
             jax.ShapeDtypeStruct((1, H, W, D), BF16),
             jax.ShapeDtypeStruct((1, H, W, D), BF16),
             jax.ShapeDtypeStruct((L, UN, UNIT, FF), BF16),
-            jax.ShapeDtypeStruct((L, NT, UN, UNIT, DH), BF16),
+            jax.ShapeDtypeStruct((L, UN, UNIT, FF), BF16),
             jax.ShapeDtypeStruct((L, R, CD, M, 8, LANES), F32),
         ),
         in_specs=[vmem] * 6 + [hbm, vmem, hbm, vmem, vmem],
         out_specs=(vmem, vmem, hbm, hbm, hbm),
         scratch_shapes=[
             V((L, J, H + 6, W + 2 * LEFT, LANES), F32),
-            V((J, H + 6, W + 2 * LEFT, LANES), F32),
+            V((L, J, H + 6, W + 2 * LEFT, LANES), F32),
             V((L, J, 49, LANES), F32),
             V((J, H, W, LANES), F32),
             V((L, D, FF), BF16),
@@ -983,11 +1112,13 @@
             V((L, N, D), F32),
             V((L, N, 1), F32),
             V((L, N, D), BF16),
+            V((L, D, N), BF16),
             V((L, NT, N, T), BF16),
-            V((L, NT, N, T), F32),
+            V((L, NT, N, T), BF16),
             V((L, N, D), F32),
             V((N, D), F32),
             V((N, D), BF16),
+            V((D, N), BF16),
             V((N, D), F32),
             V((NT, 1, T), F32),
             V((J, 1, LANES), F32),
@@ -1026,7 +1157,7 @@
     )(
         slides,
         cotangent,
-        kernel,
+        kernel.transpose(1, 2, 0, 3),
         kernel_bias,
         norm_gain,
         norm_bias,
@@ -1036,17 +1167,76 @@
         bias_out,
         layer_scale,
     )
-    output, grad_slides, low_in, low_out, small = out
-    lines = small.reshape(L, -1, J, 8, LANES).transpose(0, 1, 3, 2, 4)
-    lines = lines.reshape(L, -1, D)
+    return widen(*out, FF)
+
+
+def widen_body(output, grad_slides, low_in, low_out, small, *outs):
+    outs[0][...] = output[...]
+    outs[1][...] = grad_slides[...]
+    outs[2][...] = low_in[...].astype(F32)
+    outs[3][0] = low_out[0].astype(F32).T
+    taps, channel, bias = outs[4:]
+
+    @pl.when(pl.program_id(0) == 0)
+    def _():
+        L, D = channel.shape[1], channel.shape[2]
+        J = D // LANES
+        for l in range(L):
+            for line in range(54 + bias.shape[1] // D):
+                for j in range(J):
+                    unit = (line // 8) * J + j
+                    value = small[l, unit, line % 8 : line % 8 + 1, :]
+                    lane = j * LANES
+                    if line < 49:
+                        taps[
+                            line // 7, line % 7, l : l + 1, lane : lane + LANES
+                        ] = value
+                    elif line < 54:
+                        channel[line - 49, l : l + 1, lane : lane + LANES] = value
+                    else:
+                        lane += (line - 54) * D
+                        bias[l : l + 1, lane : lane + LANES] = value
+
+
+def widen(output, grad_slides, low_in, low_out, small, FF):
+    _, H, W, D = output.shape
+    L, DH = low_in.shape[0], low_in.shape[1] * low_in.shape[2]
+    small = small.reshape(L, -1, 8, LANES)
+    low_in = low_in.reshape(L, DH, FF)
+    low_out = low_out.reshape(L, DH, FF)
+    parts = 2
+    steps = L * parts
+    rows = -(-H // steps)
+    maps = pl.BlockSpec((1, rows, W, D), lambda i: (0, i, 0, 0))
+    wide = pl.BlockSpec((1, DH // parts, FF), lambda i: (i // parts, i % parts, 0))
+    long = pl.BlockSpec((1, FF // parts, DH), lambda i: (i // parts, i % parts, 0))
+    flat = pl.BlockSpec((1, DH, FF // parts), lambda i: (i // parts, 0, i % parts))
+
+    def whole(shape):
+        return pl.BlockSpec(shape, lambda i: (0,) * len(shape))
+
+    shapes = (
+        jax.ShapeDtypeStruct(output.shape, BF16),
+        jax.ShapeDtypeStruct(output.shape, BF16),
+        jax.ShapeDtypeStruct(low_in.shape, F32),
+        jax.ShapeDtypeStruct((L, FF, DH), F32),
+        jax.ShapeDtypeStruct((7, 7, L, D), F32),
+        jax.ShapeDtypeStruct((5, L, D), F32),
+        jax.ShapeDtypeStruct((L, FF), F32),
+    )
+    outs = pl.pallas_call(
+        widen_body,
+        grid=(steps,),
+        out_shape=shapes,
+        in_specs=[maps, maps, wide, flat, whole(small.shape)],
+        out_specs=(maps, maps, wide, long) + tuple(whole(x.shape) for x in shapes[4:]),
+        name="widen",
+    )(output, grad_slides, low_in, low_out, small)
     return (
-        output,
-        grad_slides,
-        low_in.reshape(L, DH, FF).astype(F32),
-        low_out.reshape(L, FF, DH).astype(F32),
-        lines[:, :49].reshape(L, 7, 7, D),
-        lines[:, 49:54],
-        lines[:, 54 : 54 + FF // D].reshape(L, FF),
+        *outs[:4],
+        outs[4].transpose(2, 0, 1, 3),
+        outs[5].transpose(1, 0, 2),
+        outs[6],
     )
 
 

time: 208 us -> 145 us (0.70)
  Pallas kernels: 194 us -> 143 us
  other arithmetic: 6.76 us -> 0 us
  local copies, waits for them, and re-layouts: 6.39 us -> 0 us
    pallas_call x1, Pallas kernels: 194 us -> 136 us  [per_device(): pl.pallas_call(functools.partial(step_body, sizes), out_shape=(jax.ShapeD...]
    pallas_call x0 -> x1, Pallas kernels: none -> 7.11 us  [widen(): pl.pallas_call(widen_body, grid=(steps,), out_shape=shapes, in_specs=[map...]
    convert_element_type x2 -> x0, other arithmetic: 6.76 us -> none  [the longest x1 4.28 us: per_device(): low_in.reshape(L, DH, FF).astype(F32)]
    unnamed x9 -> x0, local copies, waits for them, and re-layouts: 3.26 us -> none
where the time goes in v1:
time: 145 us; the launch traced here: 144 us
  Pallas kernels  143 us (99%)
    pallas_call x1, Pallas kernels, per_device(): pl.pallas_call(functools.partial(step_body, sizes), out_shape=(jax.ShapeD...  136 us
    pallas_call x1, Pallas kernels, widen(): pl.pallas_call(widen_body, grid=(steps,), out_shape=shapes, in_specs=[map...  7.11 us

profile of v1, /device:TPU:0, one launch (start us, length us, event | category | flops | bytes accessed | tf_op | source)
XLA Modules:
  0.0 144.3 jit_solution(15125520590105298752)
XLA Ops:
  0.6 136.4 %step.1 = (bf16[1,16,32,512]{3,2,1,0:T(8,128)(2,1)}, bf16[1,16,32,512]{3,2,1,0:T(8,128)(2,1)}, bf16[2,16,16,2048]{3,2,1,0:T(8,128)(2,1)}, bf16[2,16,16,2048]{3,2,1,0:T(8,128)(2,1)}, f32[2,4,8,1,8,128]{5,4,3,2,1,0:T(8,128)}) custom-call(bf16[1,16,32,512]{3,2,1,0:T(8,128)(2,1)} %slides.1, bf16[1,16,32,512]{3,2,1,0:T(8,128)(2,1)} %cotangent.1, ...), custom_call_target="tpu_custom_call" | custom-call | tf_op jit(solution)/shard_map/step/pallas_call | solution.py:1094
  137.0 7.1 %widen.1 = (bf16[1,16,32,512]{3,2,1,0:T(8,128)(2,1)}, bf16[1,16,32,512]{3,2,1,0:T(8,128)(2,1)}, f32[2,256,2048]{2,1,0:T(8,128)}, f32[2,2048,256]{2,1,0:T(8,128)}...) custom-call(bf16[1,16,32,512]{3,2,1,0:T(8,128)(2,1)} %get-tuple-element.19.output, ...), custom_call_target="tpu_custom_call" | custom-call | tf_op jit(solution)/shard_map/widen/pallas_call | solution.py:1227

commit v2 on v1

--- a/solution.py
+++ b/solution.py
@@ -14,6 +14,7 @@
 UNIT = 16
 LEFT = 8
 QUARTERS = 4
+PAIR = 2
 MESH = pl.DeviceIdType.MESH
 F32 = jnp.float32
 BF16 = jnp.bfloat16
@@ -64,6 +65,9 @@
     from_dp,
     from_row,
     from_col,
+    early_row,
+    early_col,
+    early_dp,
     final,
     small,
     small_row,
@@ -453,31 +457,32 @@
             out = center * scale
             normed[l, lines, :] = out
             rstd[l, lines, :] = scale
-            normal[l, lines, :] = (out * gain + shift).astype(BF16)
+            normal[lines, :] = (out * gain + shift).astype(BF16)
             return 0
 
         lax.fori_loop(0, H, norm, 0, unroll=4)
         hooks["norm"]()
-        transpose(normal.at[l], normal_t.at[l])
+        transpose(normal, normal_t.at[l])
+
+        group = hooks["group"]
 
         def expand(s, _):
             hooks["expand"](s)
-            t = my_tile(s)
-            cols = pl.ds(pl.multiple_of(t * T, T), T)
-            hidden = jnp.dot(normal[l], win[l, :, cols], preferred_element_type=F32)
-            hidden = hidden + bias_in[l : l + 1, cols]
-            square = hidden * hidden
-            tangent = jnp.tanh(hidden * (COEF + (COEF * CUBIC) * square))
-            half = 0.5 * hidden
-            both = 1.0 + tangent
-            act[l, t] = (half * both).astype(BF16)
-            rise = 0.5 * both + half * (1.0 - tangent * tangent) * (
-                COEF + (3.0 * COEF * CUBIC) * square
-            )
-            slope[l, t] = rise.astype(BF16)
+            for k in range(group):
+                t = my_tile(s * group + k)
+                cols = pl.ds(pl.multiple_of(t * T, T), T)
+                hidden = jnp.dot(normal[...], win[l, :, cols], preferred_element_type=F32)
+                hidden = hidden + bias_in[l : l + 1, cols]
+                square = hidden * hidden
+                tangent = jnp.tanh(hidden * (COEF + (COEF * CUBIC) * square))
+                both = 1.0 + tangent
+                half = 0.5 * hidden
+                act[l, t] = (half * both).astype(BF16)
+                steep = half * (COEF + (3.0 * COEF * CUBIC) * square)
+                slope[l, t] = (both * (0.5 + (1.0 - tangent) * steep)).astype(BF16)
             return 0
 
-        lax.fori_loop(0, NT, expand, 0)
+        lax.fori_loop(0, NT // group, expand, 0)
         branch[l] = jnp.broadcast_to(bias_out[l : l + 1, :], (N, D))
 
         def project(s, _):
@@ -673,6 +678,79 @@
             g_rowg(l, t, halved[-1]).wait()
         g_coreg(l, t).start()
 
+    def h_row(l, t, level):
+        b, n, halve = levels[level]
+        start, m = unit_base(level), n
+        if halve:
+            m = n // 2
+            start = start + (1 - (row // b) % 2) * m
+        return remote(
+            grads.at[l, t, core, :, pl.ds(start, m)],
+            early_row.at[t, :, pl.ds(row_slot[level], m)],
+            sem_gs.at[t, S_ROW + level],
+            sem_gr.at[l, t, S_ROW + level],
+            row=flip(row, b),
+        )
+
+    def h_row_add(l, t, level):
+        _, n, halve = levels[level]
+        m = n // 2 if halve else n
+        mine = grads.at[l, t, core, :, pl.ds(unit_base(level + 1), m)]
+        mine[...] = mine[...] + early_row[t, :, pl.ds(row_slot[level], m)]
+
+    def h_col(l, t, k):
+        peer = (col + k) % C
+        return remote(
+            grads.at[l, t, core, :, pl.ds(col_base + peer * per_col, per_col)],
+            early_col.at[t, k - 1],
+            sem_gs.at[t, S_COL + k - 1],
+            sem_gr.at[l, t, S_COL + k - 1],
+            col=peer,
+        )
+
+    my_units = pl.ds(col_base + col * per_col, per_col)
+
+    def h_dp(l, t):
+        return remote(
+            grads.at[l, t, core, 1 - dp, my_units],
+            early_dp.at[t],
+            sem_gs.at[t, S_DP],
+            sem_gr.at[l, t, S_DP],
+            dp=1 - dp,
+        )
+
+    def early_start(l, t):
+        g_core(l, t).wait()
+        mine = grads.at[l, t, core]
+        mine[...] = mine[...] + from_core[l, t]
+        for level in range(nb):
+            if level:
+                h_row(l, t, level - 1).wait()
+                h_row_add(l, t, level - 1)
+            h_row(l, t, level).start()
+
+    def early_col_go(l, t):
+        if nb:
+            h_row(l, t, nb - 1).wait()
+            h_row_add(l, t, nb - 1)
+        for k in range(1, C):
+            h_col(l, t, k).start()
+
+    def early_dp_go(l, t):
+        for k in range(1, C):
+            h_col(l, t, k).wait()
+        total = grads[l, t, core, :, my_units].astype(F32)
+        for k in range(1, C):
+            total = total + early_col[t, k - 1].astype(F32)
+        grads[l, t, core, :, my_units] = total.astype(BF16)
+        h_dp(l, t).start()
+
+    def early_colg(l, t):
+        h_dp(l, t).wait()
+        final[l, core, t, my_units] = grads[l, t, core, dp, my_units] + early_dp[t]
+        for k in range(1, C):
+            g_colg(l, t, k).start()
+
     def out_copies(l, t):
         cols = pl.ds(pl.multiple_of(t * T, T), T)
         return (
@@ -768,36 +846,50 @@
         gnorm[...] = jnp.zeros_like(gnorm)
         transpose(gb_low, gb_t)
 
-        def tile(t, _):
-            cols = pl.ds(pl.multiple_of(t * T, T), T)
-            gb = gb_low[...]
-            ga = lax.dot_general(gb, wout[l, t], COLS, preferred_element_type=F32)
-            gh = ga * slope[l, t].astype(F32)
-            gbias[t] = jnp.sum(gh, 0, keepdims=True)
-            low = gh.astype(BF16)
-            g_out = jnp.dot(gb_t[...], act[l, t], preferred_element_type=F32)
-            g_in = jnp.dot(normal_t[l], low, preferred_element_type=F32)
-            for d in range(DP):
-                grads[l, t, 0, d] = (
-                    g_in[d * DH : (d + 1) * DH].astype(BF16).reshape(UN, UNIT, T)
+        def pair(i, _):
+            first_late = 2
+            if l == L - 1:
+                first_late = 3
+
+                @pl.when(i == 2)
+                def _():
+                    for k in range(PAIR):
+                        early_start(l, k)
+
+            @pl.when(i >= first_late)
+            def _():
+                for k in range(PAIR):
+                    go_dp(l, (i - 2) * PAIR + k)
+
+            hooks('tile', i)
+            gb, gb_turned = gb_low[...], gb_t[...]
+            lows = []
+            for k in range(PAIR):
+                t = i * PAIR + k
+                ga = lax.dot_general(gb, wout[l, t], COLS, preferred_element_type=F32)
+                gh = ga * slope[l, t].astype(F32)
+                gbias[t] = jnp.sum(gh, 0, keepdims=True)
+                lows.append(gh.astype(BF16))
+            for k in range(PAIR):
+                t = i * PAIR + k
+                g_out = jnp.dot(gb_turned, act[l, t], preferred_element_type=F32)
+                grads[l, t, 1] = g_out.astype(BF16).reshape(DP, UN, UNIT, T)
+            total = gnorm[...]
+            for k in range(PAIR):
+                t = i * PAIR + k
+                g_in = jnp.dot(normal_t[l], lows[k], preferred_element_type=F32)
+                grads[l, t, 0] = g_in.astype(BF16).reshape(DP, UN, UNIT, T)
+                cols = pl.ds(pl.multiple_of(t * T, T), T)
+                total = total + lax.dot_general(
+                    lows[k], win[l, :, cols], COLS, preferred_element_type=F32
                 )
-                grads[l, t, 1, d] = (
-                    g_out[d * DH : (d + 1) * DH].astype(BF16).reshape(UN, UNIT, T)
-                )
-            g_core(l, t).start()
-            gnorm[...] += lax.dot_general(
-                low, win[l, :, cols], COLS, preferred_element_type=F32
-            )
-
-            @pl.when(t >= 2)
-            def _():
-                go_dp(l, t - 2)
-
-            hooks('tile', t)
+            gnorm[...] = total
+            for k in range(PAIR):
+                g_core(l, i * PAIR + k).start()
             return 0
 
-        lax.fori_loop(0, NT, tile, 0)
-        for t in range(NT - 2, NT):
+        lax.fori_loop(0, NT // PAIR, pair, 0)
+        for t in range(NT - 2 * PAIR, NT - PAIR):
             go_dp(l, t)
         hooks('rest', -1)
         per_line = D // T
@@ -823,6 +915,8 @@
         for k in range(3):
             put_row(l, 49 + k, jnp.sum(sums[k], 0, keepdims=True))
         halo_send(turn, gpad)
+        for t in range(NT - PAIR, NT):
+            go_dp(l, t)
         hooks('sent', -1)
         halo_recv(turn, gpad)
 
@@ -916,12 +1010,19 @@
         at(s, 1, one)
         at(s, 2, two)
         at(s, 3, three)
+        if L > 1:
+            for p in range(pieces):
+                at(s, min(1 + p, QUARTERS - 1), lambda: weights_forward(1, 0, p))
 
     def later(l):
         def in_conv(index):
             if isinstance(index, int):
-                for p in range(pieces):
-                    weights_second(l, 0, p)
+                weights_second(l, 0, pieces - 1)
+                return
+            for p in range(pieces):
+                at(index, min(1 + 3 * p, blocks - 1), lambda: weights_forward(l, 1, p))
+                if p + 1 < pieces:
+                    at(index, blocks - 2, lambda: weights_second(l, 0, p))
 
         def in_norm():
             for p in range(pieces):
@@ -931,7 +1032,7 @@
 
         def in_expand(s):
             for p in range(pieces):
-                at(s, NT // 2 + p, lambda: weights_second(l, 1, p))
+                at(s, min(1 + 2 * p, QUARTERS - 1), lambda: weights_second(l, 1, p))
 
         def in_project(s):
             def one():
@@ -946,16 +1047,25 @@
             at(s, 0, one)
             at(s, 3, three)
 
-        return dict(conv=in_conv, norm=in_norm, expand=in_expand, project=in_project)
+        return dict(
+            conv=in_conv,
+            norm=in_norm,
+            expand=in_expand,
+            project=in_project,
+            group=pieces,
+        )
 
     first = dict(
-        conv=first_conv, norm=first_norm, expand=first_expand, project=first_project
+        conv=first_conv,
+        norm=first_norm,
+        expand=first_expand,
+        project=first_project,
+        group=1,
     )
     for l in range(L):
         if l:
-            for which in range(2):
-                for p in range(pieces):
-                    weights_forward(l, which, p)
+            for p in range(pieces if l > 1 else 0):
+                weights_forward(l, 0, p)
             halo_recv(l, pads.at[l])
         forward(l, l == L - 1, later(l) if l else first)
         if l + 1 < L:
@@ -964,19 +1074,24 @@
     clock = [0.0]
     due = []
     link = [0.0]
+    serial = [0]
+    cross = [0.0]
 
     def push(ready, chain, place, arg):
-        due.append((ready, len(due), chain, place, arg))
+        serial[0] += 1
+        due.append((ready, serial[0], chain, place, arg))
 
     gchain = [
         (go_row, 4.0),
-        (go_col, 4.0),
-        (go_colg, 4.0),
+        (go_col, 4.8),
+        (go_colg, 4.8),
         (go_rowg, 4.0),
-        (go_coreg, 2.0),
+        (go_coreg, 9.0),
         (go_out, 0.0),
     ]
-    schain = [(small_second, 3.5), (small_third, 3.5), (small_fourth, 3.5), (small_end, 0)]
+    echain = [(early_col_go, 4.8), (early_dp_go, 5.4), (early_colg, 3.5)] + gchain[3:]
+    echain[2] = (early_colg, 3.5)
+    schain = [(small_second, 5.0), (small_third, 5.0), (small_fourth, 6.0), (small_end, 0)]
 
     def run_due(now):
         while due:
@@ -988,13 +1103,19 @@
             chain[place][0](*arg)
             if place + 1 < len(chain):
                 wait = chain[place][1]
-                push(max(ready, clock[0]) + wait, chain, place + 1, arg)
+                soon = max(ready, clock[0]) + wait
+                if chain is echain and place == 1:
+                    link[0] = max(link[0], clock[0]) + 0.35
+                    soon = link[0] + 3.0
+                if chain is schain and place == 0:
+                    soon = max(soon, link[0] + 4.0)
+                push(soon, chain, place + 1, arg)
 
     def spend(time):
         clock[0] += time
         run_due(clock[0])
 
-    TILE, CONV, TAP = 1.0, 0.55, 0.75
+    TILE, CONV, TAP = 1.4, 0.57, 0.75
     cut = 4
     for n, l in enumerate(reversed(range(L))):
         last = l == 0
@@ -1002,13 +1123,19 @@
         def hooks(name, index, l=l, last=last):
             if name == 'tile':
                 start = clock[0]
-                for t in range(NT):
-                    clock[0] = start + (t + 1) * TILE
+                for t in range(NT // PAIR):
+                    clock[0] = start + t * TILE
                     ready_now = [x for x in due if x[0] <= clock[0]]
                     if ready_now:
                         at(index, t, lambda: run_due(clock[0]))
+                clock[0] = start + TILE * NT // PAIR
                 for t in range(NT):
-                    begin = max(link[0], start + TILE * min(t + 3, NT))
+                    begin = start + TILE * min(t // PAIR + 2, NT // PAIR)
+                    if l == L - 1 and t < PAIR:
+                        cross[0] = max(cross[0], begin) + 2.75
+                        push(cross[0] + 2.3, echain, 0, (l, t))
+                        continue
+                    begin = max(link[0], begin)
                     link[0] = begin + 2.75
                     push(link[0] + 2.3, gchain, 0, (l, t))
             elif name == 'rest':
@@ -1019,10 +1146,10 @@
                     for k in range(1, L):
                         tap_sums(k, cut, 7, lambda q: spend(TAP))
                         small_start(k)
-                        push(clock[0] + 3.5, schain, 0, (k,))
+                        push(clock[0] + 5.0, schain, 0, (k,))
                     tap_sums(l, 0, 7, lambda q: spend(TAP))
                     small_start(l)
-                    push(clock[0] + 3.5, schain, 0, (l,))
+                    push(clock[0] + 5.0, schain, 0, (l,))
                 else:
                     tap_sums(l, 0, cut, lambda q: spend(TAP))
             elif name == 'conv':
@@ -1084,6 +1211,7 @@
         bit *= 2
         nb += 1
     per_col = count // C
+    early = PAIR
     stages = 2 + nb + 2 * (C - 1) + nb + 1
     small_peers = max(R, CD) - 1
     vmem = pl.BlockSpec(memory_space=pltpu.VMEM)
@@ -1111,7 +1239,7 @@
             V((L, NT, T, D), BF16),
             V((L, N, D), F32),
             V((L, N, 1), F32),
-            V((L, N, D), BF16),
+            V((N, D), BF16),
             V((L, D, N), BF16),
             V((L, NT, N, T), BF16),
             V((L, NT, N, T), BF16),
@@ -1127,6 +1255,9 @@
             V((L, NT, UN, UNIT, T), BF16),
             V((L, NT, max(row_units, 1), UNIT, T), BF16),
             V((L, NT, max(C - 1, 1), per_col, UNIT, T), BF16),
+            V((early, DP, max(row_units, 1), UNIT, T), BF16),
+            V((early, max(C - 1, 1), DP, per_col, UNIT, T), BF16),
+            V((early, per_col, UNIT, T), BF16),
             V((L, 2, NT, UN, UNIT, T), BF16),
             V((L, R, CD, M, 8, LANES), F32),
             V((L, max(R - 1, 1), CD, M, 8, LANES), F32),

time: 145 us -> 136 us (0.938)
  Pallas kernels: 143 us -> 135 us
    pallas_call x1, Pallas kernels: 136 us -> 128 us  [per_device(): pl.pallas_call(functools.partial(step_body, sizes), out_shape=(jax.ShapeD...]
where the time goes in v2:
time: 136 us; the launch traced here: 135 us
  Pallas kernels  135 us (99%)
    pallas_call x1, Pallas kernels, per_device(): pl.pallas_call(functools.partial(step_body, sizes), out_shape=(jax.ShapeD...  128 us
    pallas_call x1, Pallas kernels, widen(): pl.pallas_call(widen_body, grid=(steps,), out_shape=shapes, in_specs=[map...  7.11 us

profile of v2, /device:TPU:0, one launch (start us, length us, event | category | flops | bytes accessed | tf_op | source)
XLA Modules:
  0.0 135.4 jit_solution(15520556968079993170)
XLA Ops:
  0.6 127.5 %step.1 = (bf16[1,16,32,512]{3,2,1,0:T(8,128)(2,1)}, bf16[1,16,32,512]{3,2,1,0:T(8,128)(2,1)}, bf16[2,16,16,2048]{3,2,1,0:T(8,128)(2,1)}, bf16[2,16,16,2048]{3,2,1,0:T(8,128)(2,1)}, f32[2,4,8,1,8,128]{5,4,3,2,1,0:T(8,128)}) custom-call(bf16[1,16,32,512]{3,2,1,0:T(8,128)(2,1)} %slides.1, bf16[1,16,32,512]{3,2,1,0:T(8,128)(2,1)} %cotangent.1, ...), custom_call_target="tpu_custom_call" | custom-call | tf_op jit(solution)/shard_map/step/pallas_call | solution.py:1222
  128.2 7.1 %widen.1 = (bf16[1,16,32,512]{3,2,1,0:T(8,128)(2,1)}, bf16[1,16,32,512]{3,2,1,0:T(8,128)(2,1)}, f32[2,256,2048]{2,1,0:T(8,128)}, f32[2,2048,256]{2,1,0:T(8,128)}...) custom-call(bf16[1,16,32,512]{3,2,1,0:T(8,128)(2,1)} %get-tuple-element.19.output, ...), custom_call_target="tpu_custom_call" | custom-call | tf_op jit(solution)/shard_map/widen/pallas_call | solution.py:1358

commit v3 on v2

--- a/solution.py
+++ b/solution.py
@@ -36,8 +36,8 @@
     weight_out,
     bias_out,
     layer_scale,
-    output,
-    grad_slides,
+    out_map,
+    out_slides,
     out_in,
     out_out,
     out_small,
@@ -90,6 +90,9 @@
     sem_ss,
     sem_sr,
     sem_out,
+    output,
+    grad_slides,
+    sem_maps,
 ):
     R, C, DP = sizes["row"], sizes["col"], sizes["dp"]
     CD = C * DP
@@ -511,6 +514,8 @@
             return 0
 
         lax.fori_loop(0, H, finish, 0)
+        if last:
+            map_copy.start()
 
     bits = []
     bit = 2
@@ -788,6 +793,14 @@
             src, dst, sem_ss.at[stage, k - 1], sem_sr.at[l, stage, k - 1], **where
         )
 
+    def small_copy(l):
+        return pltpu.make_async_copy(
+            small_out.at[l], out_small.at[l], sem_maps.at[2 + l]
+        )
+
+    map_copy = pltpu.make_async_copy(output, out_map, sem_maps.at[0])
+    slides_copy = pltpu.make_async_copy(grad_slides, out_slides, sem_maps.at[1])
+
     def small_start(l):
         for k in range(1, R):
             s_copy(l, 0, k).start()
@@ -821,6 +834,7 @@
     def small_end(l):
         for k in range(1, R):
             s_copy(l, 3, k).wait()
+        small_copy(l).start()
 
     def backward(l, turn, hooks, last):
         gpad = gpads.at[l]
@@ -947,6 +961,8 @@
             return 0
 
         lax.fori_loop(0, H, gather, 0)
+        if last:
+            slides_copy.start()
 
     diagonals = jnp.where(row > 0, 1, 0) + jnp.where(row < R - 1, 1, 0)
     diagonals = diagonals * (
@@ -1091,7 +1107,7 @@
     ]
     echain = [(early_col_go, 4.8), (early_dp_go, 5.4), (early_colg, 3.5)] + gchain[3:]
     echain[2] = (early_colg, 3.5)
-    schain = [(small_second, 5.0), (small_third, 5.0), (small_fourth, 6.0), (small_end, 0)]
+    schain = [(small_second, 6.0), (small_third, 7.0), (small_fourth, 7.0), (small_end, 0)]
 
     def run_due(now):
         while due:
@@ -1116,7 +1132,7 @@
         run_due(clock[0])
 
     TILE, CONV, TAP = 1.4, 0.57, 0.75
-    cut = 4
+    cut = 6
     for n, l in enumerate(reversed(range(L))):
         last = l == 0
 
@@ -1146,10 +1162,10 @@
                     for k in range(1, L):
                         tap_sums(k, cut, 7, lambda q: spend(TAP))
                         small_start(k)
-                        push(clock[0] + 5.0, schain, 0, (k,))
+                        push(clock[0] + 7.0, schain, 0, (k,))
                     tap_sums(l, 0, 7, lambda q: spend(TAP))
                     small_start(l)
-                    push(clock[0] + 5.0, schain, 0, (l,))
+                    push(clock[0] + 8.0, schain, 0, (l,))
                 else:
                     tap_sums(l, 0, cut, lambda q: spend(TAP))
             elif name == 'conv':
@@ -1164,9 +1180,6 @@
     while due:
         clock[0] = max(clock[0], min(due)[0])
         run_due(clock[0])
-    for l in range(L):
-        pltpu.sync_copy(small_out.at[l], out_small.at[l])
-
     def drain(t, _):
         for l in range(L):
             for copy in out_copies(l, t):
@@ -1174,6 +1187,10 @@
         return 0
 
     lax.fori_loop(0, NT, drain, 0)
+    map_copy.wait()
+    slides_copy.wait()
+    for l in range(L):
+        small_copy(l).wait()
 
 
 def per_device(
@@ -1229,7 +1246,7 @@
             jax.ShapeDtypeStruct((L, R, CD, M, 8, LANES), F32),
         ),
         in_specs=[vmem] * 6 + [hbm, vmem, hbm, vmem, vmem],
-        out_specs=(vmem, vmem, hbm, hbm, hbm),
+        out_specs=(hbm,) * 5,
         scratch_shapes=[
             V((L, J, H + 6, W + 2 * LEFT, LANES), F32),
             V((L, J, H + 6, W + 2 * LEFT, LANES), F32),
@@ -1280,6 +1297,9 @@
             DMA((4, small_peers)),
             DMA((L, 4, small_peers)),
             DMA((2, L, NT)),
+            V((1, H, W, D), BF16),
+            V((1, H, W, D), BF16),
+            DMA((2 + L,)),
         ],
         compiler_params=pltpu.CompilerParams(
             collective_id=0, has_side_effects=True, vmem_limit_bytes=67043328

time: 136 us -> 135 us (level)
  no operation moved by 1% of the time
where the time goes in v3:
time: 135 us
  Pallas kernels  134 us (99%)
    pallas_call x1, Pallas kernels, per_device(): pl.pallas_call(functools.partial(step_body, sizes), out_shape=(jax.ShapeD...  127 us
    pallas_call x1, Pallas kernels, widen(): pl.pallas_call(widen_body, grid=(steps,), out_shape=shapes, in_specs=[map...  7.11 us

profile of v3, /device:TPU:0, one launch (start us, length us, event | category | flops | bytes accessed | tf_op | source)
XLA Modules:
  0.0 134.9 jit_solution(15479369596444171699)
XLA Ops:
  0.6 127.0 %step.1 = (bf16[1,16,32,512]{3,2,1,0:T(8,128)(2,1)}, bf16[1,16,32,512]{3,2,1,0:T(8,128)(2,1)}, bf16[2,16,16,2048]{3,2,1,0:T(8,128)(2,1)}, bf16[2,16,16,2048]{3,2,1,0:T(8,128)(2,1)}, f32[2,4,8,1,8,128]{5,4,3,2,1,0:T(8,128)}) custom-call(bf16[1,16,32,512]{3,2,1,0:T(8,128)(2,1)} %slides.1, bf16[1,16,32,512]{3,2,1,0:T(8,128)(2,1)} %cotangent.1, ...), custom_call_target="tpu_custom_call" | custom-call | tf_op jit(solution)/shard_map/step/pallas_call | solution.py:1239
  127.6 7.1 %widen.1 = (bf16[1,16,32,512]{3,2,1,0:T(8,128)(2,1)}, bf16[1,16,32,512]{3,2,1,0:T(8,128)(2,1)}, f32[2,256,2048]{2,1,0:T(8,128)}, f32[2,2048,256]{2,1,0:T(8,128)}...) custom-call(bf16[1,16,32,512]{3,2,1,0:T(8,128)(2,1)} %get-tuple-element.19.output, ...), custom_call_target="tpu_custom_call" | custom-call | tf_op jit(solution)/shard_map/widen/pallas_call | solution.py:1378
